TPU v7x, 32 devices: a whole 2x2x4 slice. The times are simulated.
32 devices in a mesh: grp: 2 (over x), dom: 16 (over z, y, core).
Axes of the slice: x: 2, y: 2, z: 4, core: 2. Of those that a mesh axis runs over, the one named last changes fastest.
Arguments:
- surplus: float32 [48, 64, 4096], P('grp', None, 'dom'), may hold values from -40 to 40
- levels: int32 [48, 3], P('grp'), may hold values from 0 to 3
Outputs:
- updated: float32 [48, 64, 4096], P('grp', None, 'dom')
- coefficients: float32 [48], replicated
All inputs are finite; a program needn't handle non-finite values.
Results may differ from a plain program's by a relative error of at most 0.0003.
Values sent between devices are 32-bit elements; how exact they have to be, the bound alone decides.
A program may use at most 64 MiB of HBM per device.

v0:
```python
import jax
import jax.numpy as jnp
from jax import lax
from jax.sharding import PartitionSpec as P


def owned(levels, count):
    indices = jnp.arange(count, dtype=jnp.int32)
    digits = jnp.stack([indices // 16, indices // 4 % 4, indices % 4])
    return jnp.all(digits[None] <= levels[:, :, None], axis=1).astype(jnp.float32)


def solve_weights(gram_matrix):
    number = gram_matrix.shape[0]
    diagonal_part = jnp.diagonal(gram_matrix) + 1e-06
    scaling = 1.0 / jnp.sqrt(diagonal_part)
    system = scaling[:, None] * gram_matrix * scaling[None, :] + 0.1 * jnp.eye(
        number, dtype=jnp.float32
    )
    factor = jnp.linalg.cholesky(system)
    target = jnp.sqrt(diagonal_part)[:, None]
    halfway = lax.linalg.triangular_solve(factor, target, left_side=True, lower=True)
    weights = lax.linalg.triangular_solve(
        factor, halfway, left_side=True, lower=True, transpose_a=True
    )
    return scaling * weights[:, 0]


def inner_rows(left_rows, right_rows):
    return lax.dot_general(
        left_rows,
        right_rows,
        (((1,), (1,)), ((), ())),
        precision=lax.Precision.HIGHEST,
        preferred_element_type=jnp.float32,
    )


def shards(surplus, levels):
    local_count = surplus.shape[0]
    subspaces = surplus.shape[1]
    grid_total = local_count * lax.axis_size("grp")
    owners = owned(levels, subspaces)
    masked = surplus * owners[:, :, None]
    flattened = masked.reshape(local_count, -1)
    portion = lax.all_gather(masked, "grp", axis=0, tiled=True)
    products = inner_rows(flattened, portion.reshape(portion.shape[0], -1))
    row_start = lax.axis_index("grp") * local_count
    placed = lax.dynamic_update_slice(
        jnp.zeros((grid_total, grid_total), jnp.float32), products, (row_start, jnp.int32(0))
    )
    gram_matrix = lax.psum(placed, ("grp", "dom"))
    coefficients = solve_weights(gram_matrix)
    own_weights = lax.dynamic_slice_in_dim(
        coefficients, lax.axis_index("grp") * local_count, local_count
    )
    partial_sum = jnp.tensordot(own_weights, masked, axes=1, precision=lax.Precision.HIGHEST)
    own_share = lax.psum_scatter(partial_sum, "grp", scatter_dimension=0, tiled=True)
    combined = lax.all_gather(own_share, "grp", axis=0, tiled=True)
    updated = owners[:, :, None] * combined[None]
    return (updated, coefficients)


def solution(mesh):
    placed = (P("grp", None, "dom"), P("grp", None))
    return jax.shard_map(
        shards, mesh=mesh, in_specs=placed, out_specs=(P("grp", None, "dom"), P()), check_vma=False
    )
```

profile of v0, /device:TPU:0, one launch (start us, length us, event | category | flops | bytes accessed | tf_op | source)
XLA Modules:
  0.0 140.4 jit_solution(13781790527731997911)
XLA Ops:
  7.2 0.0 all-gather.2.cloned.1.call-start
  7.3 0.8 compare_reduce_fusion
  8.0 0.1 copy.12
  8.1 3.5 %copy_multiply_fusion = f32[24,64,256]{2,0,1:T(8,128)} fusion(f32[24,64,256]{2,1,0:T(8,128)} %param.2, f32[24,64]{0,1:T(8,128)S(1)} %copy.12), kind=kLoop, calls=%fused_computation.1 | loop fusion | flops 393216 | bytes 3151872 | tf_op jit(solution)/shard_map/mul | solution.py:44
  11.6 0.0 copy-start
  11.6 0.0 all-gather.2.cloned.1.call-update
  11.6 0.0 reduce-scatter.2.cloned.1.call-start
  11.7 47.7 %all-gather.2.cloned.1.call-done = f32[48,64,256]{2,0,1:T(8,128)} async-done(((f32[24,64,256]{2,0,1:T(8,128)}), f32[48,64,256]{2,0,1:T(8,128)}) %all-gather.2.cloned.1.call-update) | async-done | bytes 3145744 | tf_op jit(solution)/shard_map/all_gather | solution.py:46
  59.4 0.0 copy-done
  59.4 4.5 %fusion = f32[48,48]{1,0:T(8,128)S(1)} fusion(f32[48,48]{1,0:T(8,128)S(1)} %broadcast_in_dim.5, s32[]{:T(128)S(6)} %select_n.63, f32[24,64,256]{2,0,1:T(8,128)S(1)} %copy-done, f32[48,64,256]{2,0,1:T(8,128)} %all-gather.2.cloned.1.call-done), kind=kOutput, calls=%fused_computation.3 | convolution fusion | flops 226492416 | bytes 4730884 | tf_op jit(solution)/shard_map/dot_general | solution.py:30
  63.9 39.5 %psum.7 = f32[48,48]{1,0:T(8,128)S(1)} all-reduce(f32[48,48]{1,0:T(8,128)S(1)} %fusion), channel_id=1, replica_groups=mesh['grp'=2,'dom'=16] {'grp','dom'}, use_global_device_ids=true, to_apply=%region_1.2 | all-reduce | flops 2304 | bytes 18432 | tf_op jit(solution)/shard_map/psum | solution.py:52
  103.4 1.0 gather_fusion
  104.4 0.1 select_add_fusion
  104.4 0.1 copy.14
  104.5 0.1 fusion.5
  104.6 4.4 %cholesky.16 = f32[48,48]{1,0:T(8,128)S(1)} custom-call(f32[48,48]{1,0:T(8,128)S(1)} %fusion.5), custom_call_target="Cholesky" | custom-call | tf_op jit(solution)/shard_map/jit(cholesky)/cholesky | solution.py:20
  109.0 0.6 compare_reduce_fusion.1
  109.7 0.7 fusion.2
  110.3 3.7 %custom-call.8 = f32[1,48,48]{1,2,0:T(8,128)S(1)} custom-call(f32[1,48,48]{2,1,0:T(8,128)S(1)} %fusion.2), custom_call_target="InvertDiagBlocksLowerTriangular" | custom-call | tf_op jit(solution)/shard_map/triangular_solve | solution.py:23
  114.0 0.1 convolution_bitcast_fusion.2
  114.1 0.2 fusion.1
  114.3 0.0 copy-start.1
  114.3 1.0 fusion.7
  115.3 0.6 copy.19
  115.9 0.0 reduce-scatter.2.cloned.1.call-update
  116.0 10.9 %reduce-scatter.2.cloned.1.call-done = f32[32,256]{1,0:T(8,128)} async-done(((f32[64,256]{1,0:T(8,128)}), f32[32,256]{1,0:T(8,128)}) %reduce-scatter.2.cloned.1.call-update) | async-done | bytes 32784 | tf_op jit(solution)/shard_map/reduce_scatter | solution.py:58
  126.9 4.8 %all_gather.7 = f32[64,256]{1,0:T(8,128)S(1)} all-gather(f32[32,256]{1,0:T(8,128)} %reduce-scatter.2.cloned.1.call-done), channel_id=1, replica_groups=mesh['grp'=2,'dom'=16] {'grp'}, dimensions={0}, use_global_device_ids=true | all-gather | bytes 98304 | tf_op jit(solution)/shard_map/all_gather | solution.py:59
  131.7 0.3 broadcast_multiply_fusion
  131.9 0.0 copy-done.1
  131.9 1.6 %copy.15 = f32[24,64,256]{2,1,0:T(8,128)} copy(f32[24,64,256]{2,0,1:T(8,128)S(1)} %broadcast_multiply_fusion) | data formatting | bytes 3145728
  (8 shorter events, 0.1 us)
Async XLA Ops:
  7.2 52.3 %all-gather.2.cloned.1.call-start = ((), (), s32[]{:S(2)}) async-start(), calls=%async_computation.1 | async-start | bytes 4718592 | tf_op jit(solution)/shard_map/all_gather | solution.py:46
  11.6 47.8 %copy-start = (f32[24,64,256]{2,0,1:T(8,128)S(1)}, f32[24,64,256]{2,0,1:T(8,128)}, u32[]{:S(2)}) copy-start(f32[24,64,256]{2,0,1:T(8,128)} %copy_multiply_fusion) | copy-start | bytes 4718596
  11.6 115.2 %reduce-scatter.2.cloned.1.call-start = ((), (), s32[]{:S(2)}) async-start(), calls=%async_computation.2 | async-start | bytes 98304 | tf_op jit(solution)/shard_map/reduce_scatter | solution.py:58
  114.3 17.6 %copy-start.1 = (f32[48]{0:T(128)}, f32[48]{0:T(128)S(1)}, u32[]{:S(2)}) copy-start(f32[48]{0:T(128)S(1)} %fusion.1) | copy-start | bytes 580
Sparse Core Ops, SparseCore 0:
  11.8 47.6 all-gather.1
  116.1 10.7 reduce-scatter.1
where the time goes:
time: 141 us; the launch traced here: 140 us
  waiting for transfers between devices  58.7 us (42%)
  blocking collectives  44.3 us (31%)
  other arithmetic  14.1 us (10%)
  between operations  14.1 us (10%)
  matrix products  5.76 us (4%)
  local copies, waits for them, and re-layouts  3.38 us (2%)
    all_gather x1, waiting for transfers between devices, shards(): portion = lax.all_gather(masked, 'grp', axis=0, tiled=True)  47.7 us
    psum x1, blocking collectives, shards(): gram_matrix = lax.psum(placed, ('grp', 'dom'))  39.5 us
    reduce_scatter x1, waiting for transfers between devices, shards(): lax.psum_scatter(partial_sum, 'grp', scatter_dimension=0, tiled=True)  10.9 us
    another operation x3, other arithmetic, solve_weights(): factor = jnp.linalg.cholesky(system)  5.06 us
    all_gather x1, blocking collectives, shards(): combined = lax.all_gather(own_share, 'grp', axis=0, tiled=True)  4.78 us
    dot_general x1, matrix products, inner_rows(): lax.dot_general(left_rows, right_rows, (((1,), (1,)), ((), ())), precisio...  4.46 us
    another operation x2, other arithmetic, solve_weights(): lax.linalg.triangular_solve(factor, halfway, left_side=True, lower=True,...  4.32 us
    mul x1, other arithmetic, shards(): masked = surplus * owners[:, :, None]  3.5 us
  transfers between devices with their start and end apart: 2, of which 2 were waited for; matrix products, arithmetic and copies ran while one was open for 0% of the time, Pallas kernels for 0%

commit v1 on v0

v1 whole, which is shorter than its diff:
```python
import functools

import jax
import jax.numpy as jnp
from jax import lax
from jax.experimental import pallas as pl
from jax.experimental.pallas import tpu as pltpu
from jax.sharding import PartitionSpec as P

MESH = pl.DeviceIdType.MESH
ROWS = 8
F32 = jnp.float32


def radices_of(size):
    out = []
    while size > 1:
        for r in (4, 2, 3, 5, 7, size):
            if size % r == 0:
                out.append(r)
                size //= r
                break
    return out


def split3(x):
    hi = x.astype(jnp.bfloat16)
    rest = x - hi.astype(F32)
    mid = rest.astype(jnp.bfloat16)
    lo = (rest - mid.astype(F32)).astype(jnp.bfloat16)
    return jnp.concatenate([hi, mid, lo], axis=0)


def kernel(groups, radices, local, subs, surplus, levels, comb_out, coef_out, *scratch):
    stages = len(radices)
    (xb, lev, lbc, prod, cbuf, local_sem, lev_send, lev_recv, x_send, x_recv, c_send, c_recv) = scratch[:12]
    slots = scratch[12:12 + stages]
    s_send = scratch[12 + stages:12 + 2 * stages]
    s_recv = scratch[12 + 2 * stages:12 + 3 * stages]
    grids = groups * local
    half = xb.shape[-1]
    chunks = subs // ROWS
    g = lax.axis_index("grp")
    d = lax.axis_index("dom")

    members = []
    stride = 1
    for t, r in enumerate(radices):
        digit = lax.rem(d // stride, r)
        base = d - digit * stride
        if t == 0:
            n = groups * r
            mine = g * r + digit
            device = functools.partial(lambda b, r_, q: (q // r_, b + lax.rem(q, r_)), base, r)
        else:
            n = r
            mine = digit
            device = functools.partial(lambda b, st, q: (g, b + q * st), base, stride)
        members.append((n, mine, device))
        stride *= r

    barrier = pltpu.get_barrier_semaphore()
    count = 0
    for n, mine, device in members:
        for k in range(1, n):
            q = lax.rem(mine + k, n)
            pl.semaphore_signal(barrier, inc=1, device_id=device(q), device_id_type=MESH)
            count += 1

    own_cells = pl.ds(pl.multiple_of(g * half, half), half)
    own_copy = pltpu.make_async_copy(
        surplus.at[:, :, own_cells], xb.at[pl.ds(g * local, local)], local_sem
    )
    own_copy.start()
    pl.semaphore_wait(barrier, count)

    def lev_copy(k):
        q = lax.rem(g + k, groups)
        return pltpu.make_async_remote_copy(
            src_ref=levels, dst_ref=lev.at[g], send_sem=lev_send.at[k], recv_sem=lev_recv.at[g],
            device_id=(q, d), device_id_type=MESH,
        )

    def x_copy(k, ch):
        q = lax.rem(g + k, groups)
        rows = pl.ds(pl.multiple_of(ch * ROWS, ROWS), ROWS)
        return pltpu.make_async_remote_copy(
            src_ref=surplus.at[:, rows, pl.ds(pl.multiple_of(q * half, half), half)],
            dst_ref=xb.at[pl.ds(g * local, local), rows],
            send_sem=x_send.at[k, ch], recv_sem=x_recv.at[g, ch],
            device_id=(q, d), device_id_type=MESH,
        )

    def x_arrival(k, ch):
        q = lax.rem(g + k, groups)
        rows = pl.ds(pl.multiple_of(ch * ROWS, ROWS), ROWS)
        block = xb.at[pl.ds(q * local, local), rows]
        return pltpu.make_async_remote_copy(
            src_ref=block, dst_ref=block, send_sem=x_send.at[k, ch], recv_sem=x_recv.at[q, ch],
            device_id=(q, d), device_id_type=MESH,
        )

    for k in range(1, groups):
        lev_copy(k).start()
    for ch in range(chunks):
        for k in range(1, groups):
            x_copy(k, ch).start()

    lev[g] = levels[...]
    for k in range(1, groups):
        q = lax.rem(g + k, groups)
        pltpu.make_async_remote_copy(
            src_ref=lev.at[q], dst_ref=lev.at[q], send_sem=lev_send.at[k], recv_sem=lev_recv.at[q],
            device_id=(q, d), device_id_type=MESH,
        ).wait_recv()
    for h in range(groups):
        for axis in range(3):
            lbc[axis, pl.ds(h * local, local), :] = jnp.broadcast_to(
                lev[h, :, axis:axis + 1], (local, 128)
            )
    prod[...] = jnp.zeros_like(prod)
    own_copy.wait()
    flat = xb.reshape(grids * subs, half)

    def gram_chunk(ch, carry):
        for k in range(1, groups):
            x_arrival(k, ch).wait_recv()
        lev0, lev1, lev2 = lbc[0], lbc[1], lbc[2]
        total = jnp.zeros(prod.shape, F32)
        for pair in range(0, ROWS, 2):
            parts = []
            for k in range(pair, pair + 2):
                s = ch * ROWS + k
                x = flat[pl.ds(s, grids, stride=subs), :]
                keep = (lev0 >= s // 16) & (lev1 >= lax.rem(s // 4, 4)) & (lev2 >= k % 4)
                keep = jnp.concatenate([keep] * (half // 128), axis=1) if half > 128 else keep
                parts.append(jnp.where(keep, x, 0.0))
            y = split3(jnp.concatenate(parts, axis=1))
            total += lax.dot_general(y, y, (((1,), (1,)), ((), ())), preferred_element_type=F32)
        prod[...] += total
        return carry

    lax.fori_loop(0, chunks, gram_chunk, 0)

    part = jnp.zeros((grids, grids), F32)
    for a in reversed(range(3)):
        for b in reversed(range(3)):
            part += prod[a * grids:(a + 1) * grids, b * grids:(b + 1) * grids]
    value = jnp.concatenate([part, jnp.zeros((grids, 128 - grids), F32)], axis=1)

    for t, (n, mine, device) in enumerate(members):
        buf, send, recv = slots[t], s_send[t], s_recv[t]
        buf[mine] = value
        copies = []
        for k in range(1, n):
            q = lax.rem(mine + k, n)
            copy = pltpu.make_async_remote_copy(
                src_ref=buf.at[mine], dst_ref=buf.at[mine], send_sem=send.at[k], recv_sem=recv.at[mine],
                device_id=device(q), device_id_type=MESH,
            )
            copy.start()
            copies.append(copy)
        for k in range(1, n):
            q = lax.rem(mine + k, n)
            pltpu.make_async_remote_copy(
                src_ref=buf.at[q], dst_ref=buf.at[q], send_sem=send.at[k], recv_sem=recv.at[q],
                device_id=device(q), device_id_type=MESH,
            ).wait_recv()
        value = buf[0]
        for q in range(1, n):
            value = value + buf[q]
        for copy in copies:
            copy.wait_send()

    row = lax.broadcasted_iota(jnp.int32, (grids, 128), 0)
    col = lax.broadcasted_iota(jnp.int32, (grids, 128), 1)
    eye = row == col
    diag = jnp.where(eye, value, 0.0)
    diag_col = jnp.sum(diag, axis=1, keepdims=True) + 1e-06
    diag_row = jnp.sum(diag, axis=0, keepdims=True) + 1e-06
    scale_col = 1.0 / jnp.sqrt(diag_col)
    scale_row = 1.0 / jnp.sqrt(diag_row)
    system = scale_col * value * scale_row + jnp.where(eye, 0.1, 0.0)
    system = jnp.where(col == grids, jnp.sqrt(diag_col), jnp.where(col < grids, system, 0.0))
    for k in range(grids):
        pivot_row = system[k:k + 1, :]
        inverse = 1.0 / pivot_row[:, k:k + 1]
        factor = jnp.where(row[:, 0:1] == k, 0.0, system[:, k:k + 1])
        system = system - factor * (pivot_row * inverse)
    final = jnp.sum(jnp.where(eye, system, 0.0), axis=1, keepdims=True)
    coef = scale_col * (system[:, grids:grids + 1] / final)
    coef_wide = jnp.broadcast_to(coef, (grids, 128))
    coef_out[...] = jnp.sum(jnp.where(eye, coef_wide, 0.0), axis=0, keepdims=True)[:, :grids]

    sub = lax.broadcasted_iota(jnp.int32, (subs, half), 0)
    dig0, dig1, dig2 = sub // 16, lax.rem(sub // 4, 4), lax.rem(sub, 4)
    acc = jnp.zeros((subs, half), F32)
    for i in range(grids):
        keep = (
            (lbc[0, i:i + 1, 0:1] >= dig0)
            & (lbc[1, i:i + 1, 0:1] >= dig1)
            & (lbc[2, i:i + 1, 0:1] >= dig2)
        )
        acc += jnp.where(keep, coef_wide[i:i + 1, 0:1], 0.0) * xb[i]
    cbuf[g] = acc
    for k in range(1, groups):
        q = lax.rem(g + k, groups)
        pltpu.make_async_remote_copy(
            src_ref=cbuf.at[g], dst_ref=cbuf.at[g], send_sem=c_send.at[k], recv_sem=c_recv.at[g],
            device_id=(q, d), device_id_type=MESH,
        ).start()
    for k in range(1, groups):
        q = lax.rem(g + k, groups)
        pltpu.make_async_remote_copy(
            src_ref=cbuf.at[q], dst_ref=cbuf.at[q], send_sem=c_send.at[k], recv_sem=c_recv.at[q],
            device_id=(q, d), device_id_type=MESH,
        ).wait_recv()
    for h in range(groups):
        comb_out[:, h * half:(h + 1) * half] = cbuf[h]

    for k in range(1, groups):
        q = lax.rem(g + k, groups)
        lev_copy(k).wait_send()
        for ch in range(chunks):
            x_copy(k, ch).wait_send()
        pltpu.make_async_remote_copy(
            src_ref=cbuf.at[g], dst_ref=cbuf.at[g], send_sem=c_send.at[k], recv_sem=c_recv.at[g],
            device_id=(q, d), device_id_type=MESH,
        ).wait_send()


def owned(levels, count):
    indices = jnp.arange(count, dtype=jnp.int32)
    digits = jnp.stack([indices // 16, indices // 4 % 4, indices % 4])
    return jnp.all(digits[None] <= levels[:, :, None], axis=1).astype(jnp.float32)


def shards(groups, domains, surplus, levels):
    local, subs, cells = surplus.shape
    grids = groups * local
    half = cells // groups
    radices = radices_of(domains)
    sizes = [groups * r if t == 0 else r for t, r in enumerate(radices)]
    dma = pltpu.SemaphoreType.DMA
    chunks = subs // ROWS
    combined, coefficients = pl.pallas_call(
        functools.partial(kernel, groups, radices, local, subs),
        out_shape=(
            jax.ShapeDtypeStruct((subs, cells), F32),
            jax.ShapeDtypeStruct((1, grids), F32),
        ),
        in_specs=[pl.BlockSpec(memory_space=pl.ANY), pl.BlockSpec(memory_space=pltpu.VMEM)],
        out_specs=(pl.BlockSpec(memory_space=pltpu.VMEM), pl.BlockSpec(memory_space=pltpu.VMEM)),
        scratch_shapes=[
            pltpu.VMEM((grids, subs, half), F32),
            pltpu.VMEM((groups, local, 3), jnp.int32),
            pltpu.VMEM((3, grids, 128), jnp.int32),
            pltpu.VMEM((3 * grids, 3 * grids), F32),
            pltpu.VMEM((groups, subs, half), F32),
            dma(()), dma((groups,)), dma((groups,)),
            dma((groups, chunks)), dma((groups, chunks)), dma((groups,)), dma((groups,)),
        ]
        + [pltpu.VMEM((n, grids, 128), F32) for n in sizes]
        + [dma((n,)) for n in sizes]
        + [dma((n,)) for n in sizes],
        compiler_params=pltpu.CompilerParams(collective_id=0, has_side_effects=True),
    )(surplus, levels)
    owners = owned(levels, subs)
    updated = owners[:, :, None] * combined[None]
    return (updated, coefficients.reshape(grids))


def solution(mesh):
    placed = (P("grp", None, "dom"), P("grp", None))
    return jax.shard_map(
        functools.partial(shards, mesh.shape["grp"], mesh.shape["dom"]),
        mesh=mesh, in_specs=placed, out_specs=(P("grp", None, "dom"), P()), check_vma=False,
    )
```

time: 141 us -> 47.6 us (0.34)
  waiting for transfers between devices: 58.7 us -> 0 us
  blocking collectives: 44.3 us -> 0 us
  Pallas kernels: 0 us -> 41.7 us
  between operations: 14.1 us -> 0.68 us
  other arithmetic: 14.1 us -> 3.05 us
  matrix products: 5.76 us -> 0 us
  local copies, waits for them, and re-layouts: 3.38 us -> 1.88 us
    all_gather x1 -> x0, waiting for transfers between devices: 47.7 us -> none  [shards(): portion = lax.all_gather(masked, 'grp', axis=0, tiled=True)]
    pallas_call x0 -> x1, Pallas kernels: none -> 41.7 us  [shards(): pl.pallas_call(functools.partial(kernel, groups, radices, local, subs), o...]
    psum x1 -> x0, blocking collectives: 39.5 us -> none  [shards(): gram_matrix = lax.psum(placed, ('grp', 'dom'))]
    reduce_scatter x1 -> x0, waiting for transfers between devices: 10.9 us -> none  [shards(): lax.psum_scatter(partial_sum, 'grp', scatter_dimension=0, tiled=True)]
    another operation x5 -> x0, other arithmetic: 9.38 us -> none  [the longest x3 5.06 us: solve_weights(): factor = jnp.linalg.cholesky(system)]
    dot_general x2 -> x0, matrix products: 5.45 us -> none  [the longest x1 4.46 us: inner_rows(): lax.dot_general(left_rows, right_rows, (((1,), (1,)), ((), ())), precisio...]
    all_gather x1 -> x0, blocking collectives: 4.78 us -> none  [shards(): combined = lax.all_gather(own_share, 'grp', axis=0, tiled=True)]
    mul x1 -> x0, other arithmetic: 3.5 us -> none  [shards(): masked = surplus * owners[:, :, None]]
  transfers between devices with their start and end apart: 2 -> 0, of which waited for: 2 -> 0; matrix products, arithmetic and copies ran while one was open for 0% -> 0% of each run, Pallas kernels for 0% -> 0%
where the time goes in v1:
time: 47.6 us; the launch traced here: 47.4 us
  Pallas kernels  41.7 us (88%)
  other arithmetic  3.05 us (6%)
  local copies, waits for them, and re-layouts  1.88 us (4%)
  between operations  0.68 us (1%)
    pallas_call x1, Pallas kernels, shards(): pl.pallas_call(functools.partial(kernel, groups, radices, local, subs), o...  41.7 us
    mul x1, other arithmetic, shards(): updated = owners[:, :, None] * combined[None]  2.25 us
    unnamed x4, local copies, waits for them, and re-layouts  1.88 us

profile of v1, /device:TPU:0, one launch (start us, length us, event | category | flops | bytes accessed | tf_op | source)
XLA Modules:
  0.0 47.4 jit_solution(3610187572736573714)
XLA Ops:
  0.7 0.8 %compare_reduce_fusion = pred[24,64]{1,0:T(8,128)(4,1)S(1)} fusion(s32[24,3]{0,1:T(4,128)} %param.3, s32[3,64]{1,0:T(4,128)S(1)} %pad_add_fusion), kind=kLoop, calls=%fused_computation.1 | loop fusion | flops 7680 | bytes 2592 | tf_op jit(solution)/shard_map/reduce_and | solution.py:235
  1.5 1.4 %copy.6.levels = s32[24,3]{1,0:T(8,128)} copy(s32[24,3]{0,1:T(4,128)} %param.3) | data formatting | bytes 576 | tf_op args[1]
  2.8 41.7 %shard_map.41 = (f32[64,256]{1,0:T(8,128)}, f32[1,48]{1,0:T(1,128)}) custom-call(f32[24,64,256]{2,1,0:T(8,128)} %surplus.1, s32[24,3]{1,0:T(8,128)} %copy.6.levels), custom_call_target="tpu_custom_call" | custom-call | tf_op jit(solution)/shard_map/pallas_call | solution.py:246
  44.6 0.0 copy-start
  44.6 2.3 %broadcast_multiply_fusion = f32[24,64,256]{2,1,0:T(8,128)} fusion(f32[64,256]{1,0:T(8,128)} %get-tuple-element.4, f32[24,64]{1,0:T(8,128)S(1)} %convert_element_type.7), kind=kLoop, calls=%fused_computation | loop fusion | flops 393216 | bytes 1644544 | tf_op jit(solution)/shard_map/mul | solution.py:269
  46.8 0.0 copy-done
  46.8 0.5 %copy.8 = f32[48]{0:T(128)} copy(f32[48]{0:T(128)S(1)} %bitcast.1) | data formatting | bytes 384
  (4 shorter events, 0.0 us)
Async XLA Ops:
  44.6 2.3 %copy-start = (f32[1,48]{1,0:T(1,128)S(1)}, f32[1,48]{1,0:T(1,128)}, u32[]{:S(2)}) copy-start(f32[1,48]{1,0:T(1,128)} %get-tuple-element.5) | copy-start | bytes 580

commit v2 on v1

--- a/solution.py
+++ b/solution.py
@@ -9,6 +9,8 @@
 
 MESH = pl.DeviceIdType.MESH
 ROWS = 8
+BLOCK = 4
+SPREAD = 4
 F32 = jnp.float32
 
 
@@ -23,6 +25,10 @@
     return out
 
 
+def digits_of(sub):
+    return (sub // 16).astype(F32), lax.rem(sub // 4, 4).astype(F32), lax.rem(sub, 4).astype(F32)
+
+
 def split3(x):
     hi = x.astype(jnp.bfloat16)
     rest = x - hi.astype(F32)
@@ -31,7 +37,7 @@
     return jnp.concatenate([hi, mid, lo], axis=0)
 
 
-def kernel(groups, radices, local, subs, surplus, levels, comb_out, coef_out, *scratch):
+def kernel(groups, radices, local, subs, surplus, levels, comb_out, coef_out, lev_out, *scratch):
     stages = len(radices)
     (xb, lev, lbc, prod, cbuf, local_sem, lev_send, lev_recv, x_send, x_recv, c_send, c_recv) = scratch[:12]
     slots = scratch[12:12 + stages]
@@ -113,11 +119,15 @@
             src_ref=lev.at[q], dst_ref=lev.at[q], send_sem=lev_send.at[k], recv_sem=lev_recv.at[q],
             device_id=(q, d), device_id_type=MESH,
         ).wait_recv()
+    lev_eye = lax.broadcasted_iota(jnp.int32, (local, local), 0) == lax.broadcasted_iota(
+        jnp.int32, (local, local), 1
+    )
     for h in range(groups):
         for axis in range(3):
-            lbc[axis, pl.ds(h * local, local), :] = jnp.broadcast_to(
-                lev[h, :, axis:axis + 1], (local, 128)
-            )
+            lev_row = lev[h, axis:axis + 1, :].astype(F32)
+            lev_col = jnp.sum(jnp.where(lev_eye, lev_row, 0.0), axis=1, keepdims=True)
+            lbc[axis, pl.ds(h * local, local), :] = jnp.broadcast_to(lev_col, (local, 128))
+    lev_out[...] = lbc[:, pl.ds(pl.multiple_of(g * local, 8), local), :]
     prod[...] = jnp.zeros_like(prod)
     own_copy.wait()
     flat = xb.reshape(grids * subs, half)
@@ -132,7 +142,11 @@
             for k in range(pair, pair + 2):
                 s = ch * ROWS + k
                 x = flat[pl.ds(s, grids, stride=subs), :]
-                keep = (lev0 >= s // 16) & (lev1 >= lax.rem(s // 4, 4)) & (lev2 >= k % 4)
+                keep = (
+                    (lev0 >= (s // 16).astype(F32))
+                    & (lev1 >= lax.rem(s // 4, 4).astype(F32))
+                    & (lev2 >= float(k % 4))
+                )
                 keep = jnp.concatenate([keep] * (half // 128), axis=1) if half > 128 else keep
                 parts.append(jnp.where(keep, x, 0.0))
             y = split3(jnp.concatenate(parts, axis=1))
@@ -147,6 +161,8 @@
         for b in reversed(range(3)):
             part += prod[a * grids:(a + 1) * grids, b * grids:(b + 1) * grids]
     value = jnp.concatenate([part, jnp.zeros((grids, 128 - grids), F32)], axis=1)
+    fold = grids // 2
+    value = value[:fold] + pltpu.roll(value[fold:], 64, 1)
 
     for t, (n, mine, device) in enumerate(members):
         buf, send, recv = slots[t], s_send[t], s_recv[t]
@@ -172,6 +188,11 @@
         for copy in copies:
             copy.wait_send()
 
+    left = lax.broadcasted_iota(jnp.int32, (fold, 128), 1) < 64
+    value = jnp.concatenate(
+        [jnp.where(left, value, 0.0), jnp.where(left, pltpu.roll(value, 64, 1), 0.0)], axis=0
+    )
+
     row = lax.broadcasted_iota(jnp.int32, (grids, 128), 0)
     col = lax.broadcasted_iota(jnp.int32, (grids, 128), 1)
     eye = row == col
@@ -182,18 +203,27 @@
     scale_row = 1.0 / jnp.sqrt(diag_row)
     system = scale_col * value * scale_row + jnp.where(eye, 0.1, 0.0)
     system = jnp.where(col == grids, jnp.sqrt(diag_col), jnp.where(col < grids, system, 0.0))
-    for k in range(grids):
-        pivot_row = system[k:k + 1, :]
-        inverse = 1.0 / pivot_row[:, k:k + 1]
-        factor = jnp.where(row[:, 0:1] == k, 0.0, system[:, k:k + 1])
-        system = system - factor * (pivot_row * inverse)
+    for first in range(0, grids, BLOCK):
+        width = min(BLOCK, grids - first)
+        rows = [system[first + j:first + j + 1, :] for j in range(width)]
+        cols = [
+            jnp.broadcast_to(system[:, first + j:first + j + 1], (grids, 128)) for j in range(width)
+        ]
+        for j in range(width):
+            k = first + j
+            inverse = 1.0 / cols[j][k:k + 1, :]
+            factor = jnp.where(row == k, 0.0, cols[j] * inverse)
+            for m in range(j + 1, width):
+                cols[m] = cols[m] - factor * cols[m][k:k + 1, :]
+                rows[m] = rows[m] - factor[first + m:first + m + 1, :] * rows[j]
+            system = system - factor * rows[j]
     final = jnp.sum(jnp.where(eye, system, 0.0), axis=1, keepdims=True)
     coef = scale_col * (system[:, grids:grids + 1] / final)
     coef_wide = jnp.broadcast_to(coef, (grids, 128))
     coef_out[...] = jnp.sum(jnp.where(eye, coef_wide, 0.0), axis=0, keepdims=True)[:, :grids]
 
     sub = lax.broadcasted_iota(jnp.int32, (subs, half), 0)
-    dig0, dig1, dig2 = sub // 16, lax.rem(sub // 4, 4), lax.rem(sub, 4)
+    dig0, dig1, dig2 = digits_of(sub)
     acc = jnp.zeros((subs, half), F32)
     for i in range(grids):
         keep = (
@@ -229,10 +259,23 @@
         ).wait_send()
 
 
-def owned(levels, count):
-    indices = jnp.arange(count, dtype=jnp.int32)
-    digits = jnp.stack([indices // 16, indices // 4 % 4, indices % 4])
-    return jnp.all(digits[None] <= levels[:, :, None], axis=1).astype(jnp.float32)
+def spread(combined, coef, lev, updated, coef_out, block, sems):
+    local, subs, cells = updated.shape
+    coef_out[...] = coef[...]
+    dig0, dig1, dig2 = digits_of(lax.broadcasted_iota(jnp.int32, (subs, 128), 0))
+    copies = []
+    for i in range(local):
+        keep = (lev[0, i:i + 1, :] >= dig0) & (lev[1, i:i + 1, :] >= dig1) & (lev[2, i:i + 1, :] >= dig2)
+        for c in range(0, cells, 128):
+            block[i, :, c:c + 128] = jnp.where(keep, combined[:, c:c + 128], 0.0)
+        if (i + 1) % SPREAD == 0 or i + 1 == local:
+            n = len(copies)
+            part = pl.ds(n * SPREAD, i + 1 - n * SPREAD)
+            copy = pltpu.make_async_copy(block.at[part], updated.at[part], sems.at[n])
+            copy.start()
+            copies.append(copy)
+    for copy in copies:
+        copy.wait()
 
 
 def shards(groups, domains, surplus, levels):
@@ -243,30 +286,39 @@
     sizes = [groups * r if t == 0 else r for t, r in enumerate(radices)]
     dma = pltpu.SemaphoreType.DMA
     chunks = subs // ROWS
-    combined, coefficients = pl.pallas_call(
+    combined, coefficients, lev_wide = pl.pallas_call(
         functools.partial(kernel, groups, radices, local, subs),
         out_shape=(
             jax.ShapeDtypeStruct((subs, cells), F32),
             jax.ShapeDtypeStruct((1, grids), F32),
+            jax.ShapeDtypeStruct((3, local, 128), F32),
         ),
         in_specs=[pl.BlockSpec(memory_space=pl.ANY), pl.BlockSpec(memory_space=pltpu.VMEM)],
-        out_specs=(pl.BlockSpec(memory_space=pltpu.VMEM), pl.BlockSpec(memory_space=pltpu.VMEM)),
+        out_specs=tuple(pl.BlockSpec(memory_space=pltpu.VMEM) for _ in range(3)),
         scratch_shapes=[
             pltpu.VMEM((grids, subs, half), F32),
-            pltpu.VMEM((groups, local, 3), jnp.int32),
-            pltpu.VMEM((3, grids, 128), jnp.int32),
+            pltpu.VMEM((groups, 3, local), jnp.int32),
+            pltpu.VMEM((3, grids, 128), F32),
             pltpu.VMEM((3 * grids, 3 * grids), F32),
             pltpu.VMEM((groups, subs, half), F32),
             dma(()), dma((groups,)), dma((groups,)),
             dma((groups, chunks)), dma((groups, chunks)), dma((groups,)), dma((groups,)),
         ]
-        + [pltpu.VMEM((n, grids, 128), F32) for n in sizes]
+        + [pltpu.VMEM((n, grids // 2, 128), F32) for n in sizes]
         + [dma((n,)) for n in sizes]
         + [dma((n,)) for n in sizes],
         compiler_params=pltpu.CompilerParams(collective_id=0, has_side_effects=True),
-    )(surplus, levels)
-    owners = owned(levels, subs)
-    updated = owners[:, :, None] * combined[None]
+    )(surplus, levels.T)
+    updated, coefficients = pl.pallas_call(
+        spread,
+        out_shape=(
+            jax.ShapeDtypeStruct((local, subs, cells), F32),
+            jax.ShapeDtypeStruct((1, grids), F32),
+        ),
+        in_specs=[pl.BlockSpec(memory_space=pltpu.VMEM)] * 3,
+        out_specs=(pl.BlockSpec(memory_space=pl.ANY), pl.BlockSpec(memory_space=pltpu.VMEM)),
+        scratch_shapes=[pltpu.VMEM((local, subs, cells), F32), dma((-(-local // SPREAD),))],
+    )(combined, coefficients, lev_wide)
     return (updated, coefficients.reshape(grids))
 
 

time: 47.6 us -> 42.4 us (0.89)
  other arithmetic: 3.05 us -> 0 us
  local copies, waits for them, and re-layouts: 1.88 us -> 0 us
    pallas_call x1, Pallas kernels: 41.7 us -> 39 us  [shards(): pl.pallas_call(functools.partial(kernel, groups, radices, local, subs), o...]
    pallas_call x0 -> x1, Pallas kernels: none -> 2.59 us  [shards(): pl.pallas_call(spread, out_shape=(jax.ShapeDtypeStruct((local, subs, cell...]
    mul x1 -> x0, other arithmetic: 2.25 us -> none  [shards(): updated = owners[:, :, None] * combined[None]]
    unnamed x4 -> x0, local copies, waits for them, and re-layouts: 1.88 us -> none
    reduce_and x1 -> x0, other arithmetic: 0.76 us -> none  [owned(): jnp.all(digits[None] <= levels[:, :, None], axis=1).astype(jnp.float32)]
where the time goes in v2:
time: 42.4 us; the launch traced here: 42.2 us
  Pallas kernels  41.6 us (98%)
  between operations  0.64 us (2%)
    pallas_call x1, Pallas kernels, shards(): pl.pallas_call(functools.partial(kernel, groups, radices, local, subs), o...  39 us
    pallas_call x1, Pallas kernels, shards(): pl.pallas_call(spread, out_shape=(jax.ShapeDtypeStruct((local, subs, cell...  2.59 us

profile of v2, /device:TPU:0, one launch (start us, length us, event | category | flops | bytes accessed | tf_op | source)
XLA Modules:
  0.0 42.2 jit_solution(3583446378676042806)
XLA Ops:
  0.6 39.0 %shard_map.41 = (f32[64,256]{1,0:T(8,128)}, f32[1,48]{1,0:T(1,128)}, f32[3,24,128]{2,1,0:T(8,128)}) custom-call(f32[24,64,256]{2,1,0:T(8,128)} %surplus.1, s32[3,24]{1,0:T(4,128)} %bitcast.2), custom_call_target="tpu_custom_call" | custom-call | tf_op jit(solution)/shard_map/pallas_call | solution.py:289
  39.6 2.6 %shard_map.42 = (f32[24,64,256]{2,1,0:T(8,128)}, f32[1,48]{1,0:T(1,128)}) custom-call(f32[64,256]{1,0:T(8,128)} %get-tuple-element.7.combined, f32[1,48]{1,0:T(1,128)} %get-tuple-element.8.coef, f32[3,24,128]{2,1,0:T(8,128)} %get-tuple-element.9.lev), custom_call_target="tpu_custom_call" | custom-call | tf_op jit(solution)/shard_map/pallas_call | solution.py:312

commit v3 on v2

--- a/solution.py
+++ b/solution.py
@@ -9,7 +9,8 @@
 
 MESH = pl.DeviceIdType.MESH
 ROWS = 8
-BLOCK = 4
+BLOCK = 8
+PIECES = 2
 SPREAD = 4
 F32 = jnp.float32
 
@@ -27,6 +28,16 @@
 
 def digits_of(sub):
     return (sub // 16).astype(F32), lax.rem(sub // 4, 4).astype(F32), lax.rem(sub, 4).astype(F32)
+
+
+def partner(mine, k, n):
+    if n & (n - 1):
+        return lax.rem(mine + k, n)
+    other, bit = 0, 1
+    while bit < n:
+        other = other + lax.rem(lax.rem(mine // bit, 2) + (k // bit) % 2, 2) * bit
+        bit *= 2
+    return other
 
 
 def split3(x):
@@ -69,7 +80,7 @@
     count = 0
     for n, mine, device in members:
         for k in range(1, n):
-            q = lax.rem(mine + k, n)
+            q = partner(mine, k, n)
             pl.semaphore_signal(barrier, inc=1, device_id=device(q), device_id_type=MESH)
             count += 1
 
@@ -156,20 +167,18 @@
 
     lax.fori_loop(0, chunks, gram_chunk, 0)
 
-    part = jnp.zeros((grids, grids), F32)
-    for a in reversed(range(3)):
-        for b in reversed(range(3)):
-            part += prod[a * grids:(a + 1) * grids, b * grids:(b + 1) * grids]
+    part = prod[2 * grids:, :] + prod[grids:2 * grids, :] + prod[:grids, :]
+    part = part[:, 2 * grids:] + part[:, grids:2 * grids] + part[:, :grids]
     value = jnp.concatenate([part, jnp.zeros((grids, 128 - grids), F32)], axis=1)
     fold = grids // 2
     value = value[:fold] + pltpu.roll(value[fold:], 64, 1)
 
+    copies = []
     for t, (n, mine, device) in enumerate(members):
         buf, send, recv = slots[t], s_send[t], s_recv[t]
         buf[mine] = value
-        copies = []
-        for k in range(1, n):
-            q = lax.rem(mine + k, n)
+        for k in reversed(range(1, n)):
+            q = partner(mine, k, n)
             copy = pltpu.make_async_remote_copy(
                 src_ref=buf.at[mine], dst_ref=buf.at[mine], send_sem=send.at[k], recv_sem=recv.at[mine],
                 device_id=device(q), device_id_type=MESH,
@@ -177,7 +186,7 @@
             copy.start()
             copies.append(copy)
         for k in range(1, n):
-            q = lax.rem(mine + k, n)
+            q = partner(mine, k, n)
             pltpu.make_async_remote_copy(
                 src_ref=buf.at[q], dst_ref=buf.at[q], send_sem=send.at[k], recv_sem=recv.at[q],
                 device_id=device(q), device_id_type=MESH,
@@ -185,8 +194,6 @@
         value = buf[0]
         for q in range(1, n):
             value = value + buf[q]
-        for copy in copies:
-            copy.wait_send()
 
     left = lax.broadcasted_iota(jnp.int32, (fold, 128), 1) < 64
     value = jnp.concatenate(
@@ -222,41 +229,43 @@
     coef_wide = jnp.broadcast_to(coef, (grids, 128))
     coef_out[...] = jnp.sum(jnp.where(eye, coef_wide, 0.0), axis=0, keepdims=True)[:, :grids]
 
-    sub = lax.broadcasted_iota(jnp.int32, (subs, half), 0)
-    dig0, dig1, dig2 = digits_of(sub)
-    acc = jnp.zeros((subs, half), F32)
-    for i in range(grids):
-        keep = (
-            (lbc[0, i:i + 1, 0:1] >= dig0)
-            & (lbc[1, i:i + 1, 0:1] >= dig1)
-            & (lbc[2, i:i + 1, 0:1] >= dig2)
+    piece = subs // PIECES
+
+    def c_copy(slot, k, p):
+        block = cbuf.at[slot, pl.ds(p * piece, piece)]
+        return pltpu.make_async_remote_copy(
+            src_ref=block, dst_ref=block, send_sem=c_send.at[k, p], recv_sem=c_recv.at[slot, p],
+            device_id=(lax.rem(g + k, groups), d), device_id_type=MESH,
         )
-        acc += jnp.where(keep, coef_wide[i:i + 1, 0:1], 0.0) * xb[i]
-    cbuf[g] = acc
-    for k in range(1, groups):
-        q = lax.rem(g + k, groups)
-        pltpu.make_async_remote_copy(
-            src_ref=cbuf.at[g], dst_ref=cbuf.at[g], send_sem=c_send.at[k], recv_sem=c_recv.at[g],
-            device_id=(q, d), device_id_type=MESH,
-        ).start()
-    for k in range(1, groups):
-        q = lax.rem(g + k, groups)
-        pltpu.make_async_remote_copy(
-            src_ref=cbuf.at[q], dst_ref=cbuf.at[q], send_sem=c_send.at[k], recv_sem=c_recv.at[q],
-            device_id=(q, d), device_id_type=MESH,
-        ).wait_recv()
+
+    for p in range(PIECES):
+        sub = lax.broadcasted_iota(jnp.int32, (piece, half), 0) + p * piece
+        dig0, dig1, dig2 = digits_of(sub)
+        acc = jnp.zeros((piece, half), F32)
+        for i in range(grids):
+            keep = (
+                (lbc[0, i:i + 1, 0:1] >= dig0)
+                & (lbc[1, i:i + 1, 0:1] >= dig1)
+                & (lbc[2, i:i + 1, 0:1] >= dig2)
+            )
+            acc += jnp.where(keep, coef_wide[i:i + 1, 0:1], 0.0) * xb[i, p * piece:(p + 1) * piece]
+        cbuf[g, p * piece:(p + 1) * piece] = acc
+        for k in range(1, groups):
+            c_copy(g, k, p).start()
+    for p in range(PIECES):
+        for k in range(1, groups):
+            c_copy(lax.rem(g + k, groups), k, p).wait_recv()
     for h in range(groups):
         comb_out[:, h * half:(h + 1) * half] = cbuf[h]
 
+    for copy in copies:
+        copy.wait_send()
     for k in range(1, groups):
-        q = lax.rem(g + k, groups)
         lev_copy(k).wait_send()
         for ch in range(chunks):
             x_copy(k, ch).wait_send()
-        pltpu.make_async_remote_copy(
-            src_ref=cbuf.at[g], dst_ref=cbuf.at[g], send_sem=c_send.at[k], recv_sem=c_recv.at[g],
-            device_id=(q, d), device_id_type=MESH,
-        ).wait_send()
+        for p in range(PIECES):
+            c_copy(g, k, p).wait_send()
 
 
 def spread(combined, coef, lev, updated, coef_out, block, sems):
@@ -302,7 +311,7 @@
             pltpu.VMEM((3 * grids, 3 * grids), F32),
             pltpu.VMEM((groups, subs, half), F32),
             dma(()), dma((groups,)), dma((groups,)),
-            dma((groups, chunks)), dma((groups, chunks)), dma((groups,)), dma((groups,)),
+            dma((groups, chunks)), dma((groups, chunks)), dma((groups, PIECES)), dma((groups, PIECES)),
         ]
         + [pltpu.VMEM((n, grids // 2, 128), F32) for n in sizes]
         + [dma((n,)) for n in sizes]

time: 42.4 us -> 41.9 us (0.988)
  Pallas kernels: 41.6 us -> 41.1 us
    pallas_call x1, Pallas kernels: 39 us -> 38.5 us  [shards(): pl.pallas_call(functools.partial(kernel, groups, radices, local, subs), o...]
where the time goes in v3:
time: 41.9 us; the launch traced here: 41.7 us
  Pallas kernels  41.1 us (98%)
  between operations  0.64 us (2%)
    pallas_call x1, Pallas kernels, shards(): pl.pallas_call(functools.partial(kernel, groups, radices, local, subs), o...  38.5 us
    pallas_call x1, Pallas kernels, shards(): pl.pallas_call(spread, out_shape=(jax.ShapeDtypeStruct((local, subs, cell...  2.59 us

profile of v3, /device:TPU:0, one launch (start us, length us, event | category | flops | bytes accessed | tf_op | source)
XLA Modules:
  0.0 41.7 jit_solution(3085870922029769678)
XLA Ops:
  0.6 38.5 %shard_map.41 = (f32[64,256]{1,0:T(8,128)}, f32[1,48]{1,0:T(1,128)}, f32[3,24,128]{2,1,0:T(8,128)}) custom-call(f32[24,64,256]{2,1,0:T(8,128)} %surplus.1, s32[3,24]{1,0:T(4,128)} %bitcast.2), custom_call_target="tpu_custom_call" | custom-call | tf_op jit(solution)/shard_map/pallas_call | solution.py:298
  39.1 2.6 %shard_map.42 = (f32[24,64,256]{2,1,0:T(8,128)}, f32[1,48]{1,0:T(1,128)}) custom-call(f32[64,256]{1,0:T(8,128)} %get-tuple-element.7.combined, f32[1,48]{1,0:T(1,128)} %get-tuple-element.8.coef, f32[3,24,128]{2,1,0:T(8,128)} %get-tuple-element.9.lev), custom_call_target="tpu_custom_call" | custom-call | tf_op jit(solution)/shard_map/pallas_call | solution.py:321

commit v4 on v3

--- a/solution.py
+++ b/solution.py
@@ -9,7 +9,7 @@
 
 MESH = pl.DeviceIdType.MESH
 ROWS = 8
-BLOCK = 8
+BLOCK = 16
 PIECES = 2
 SPREAD = 4
 F32 = jnp.float32
@@ -28,16 +28,6 @@
 
 def digits_of(sub):
     return (sub // 16).astype(F32), lax.rem(sub // 4, 4).astype(F32), lax.rem(sub, 4).astype(F32)
-
-
-def partner(mine, k, n):
-    if n & (n - 1):
-        return lax.rem(mine + k, n)
-    other, bit = 0, 1
-    while bit < n:
-        other = other + lax.rem(lax.rem(mine // bit, 2) + (k // bit) % 2, 2) * bit
-        bit *= 2
-    return other
 
 
 def split3(x):
@@ -80,7 +70,7 @@
     count = 0
     for n, mine, device in members:
         for k in range(1, n):
-            q = partner(mine, k, n)
+            q = lax.rem(mine + k, n)
             pl.semaphore_signal(barrier, inc=1, device_id=device(q), device_id_type=MESH)
             count += 1
 
@@ -177,8 +167,8 @@
     for t, (n, mine, device) in enumerate(members):
         buf, send, recv = slots[t], s_send[t], s_recv[t]
         buf[mine] = value
-        for k in reversed(range(1, n)):
-            q = partner(mine, k, n)
+        for k in range(1, n):
+            q = lax.rem(mine + k, n)
             copy = pltpu.make_async_remote_copy(
                 src_ref=buf.at[mine], dst_ref=buf.at[mine], send_sem=send.at[k], recv_sem=recv.at[mine],
                 device_id=device(q), device_id_type=MESH,
@@ -186,7 +176,7 @@
             copy.start()
             copies.append(copy)
         for k in range(1, n):
-            q = partner(mine, k, n)
+            q = lax.rem(mine + k, n)
             pltpu.make_async_remote_copy(
                 src_ref=buf.at[q], dst_ref=buf.at[q], send_sem=send.at[k], recv_sem=recv.at[q],
                 device_id=device(q), device_id_type=MESH,

time: 41.9 us -> 41.6 us (level)
  no operation moved by 1% of the time
where the time goes in v4:
time: 41.6 us; the launch traced here: 41.4 us
  Pallas kernels  40.8 us (98%)
  between operations  0.64 us (2%)
    pallas_call x1, Pallas kernels, shards(): pl.pallas_call(functools.partial(kernel, groups, radices, local, subs), o...  38.2 us
    pallas_call x1, Pallas kernels, shards(): pl.pallas_call(spread, out_shape=(jax.ShapeDtypeStruct((local, subs, cell...  2.59 us

profile of v4, /device:TPU:0, one launch (start us, length us, event | category | flops | bytes accessed | tf_op | source)
XLA Modules:
  0.0 41.4 jit_solution(13250639285950382694)
XLA Ops:
  0.6 38.2 %shard_map.41 = (f32[64,256]{1,0:T(8,128)}, f32[1,48]{1,0:T(1,128)}, f32[3,24,128]{2,1,0:T(8,128)}) custom-call(f32[24,64,256]{2,1,0:T(8,128)} %surplus.1, s32[3,24]{1,0:T(4,128)} %bitcast.2), custom_call_target="tpu_custom_call" | custom-call | tf_op jit(solution)/shard_map/pallas_call | solution.py:288
  38.8 2.6 %shard_map.42 = (f32[24,64,256]{2,1,0:T(8,128)}, f32[1,48]{1,0:T(1,128)}) custom-call(f32[64,256]{1,0:T(8,128)} %get-tuple-element.7.combined, f32[1,48]{1,0:T(1,128)} %get-tuple-element.8.coef, f32[3,24,128]{2,1,0:T(8,128)} %get-tuple-element.9.lev), custom_call_target="tpu_custom_call" | custom-call | tf_op jit(solution)/shard_map/pallas_call | solution.py:311
